TPU v7x, 1024 devices: a whole 8x8x8 slice. The times are simulated.
1024 devices in a mesh: rows: 32 (over y_hi, x), cols: 4 (over y_lo, core), reps: 8 (over z).
Axes of the slice: x: 8, y: 8 (y_hi: 4, y_lo: 2; y = y_hi * 2 + y_lo), z: 8, core: 2. Of those that a mesh axis runs over, the one named last changes fastest.
Arguments:
- features: bfloat16 [32768, 512], P('rows', 'cols'), may hold values from -6 to 6
- tiles: bfloat16 [65536, 128, 128], P(('rows', 'reps')), may hold values from -0.1875 to 0.1875
- tile_cols: int32 [256, 256], P(('rows', 'reps')), may hold values from 0 to 255, as said below
- tile_ptr: int32 [256, 33], P(('rows', 'reps')), may hold values from 0 to 256, as said below
Outputs:
- aggregated: bfloat16 [32768, 512], P(('rows', 'reps'), 'cols')
Inputs may be any that keep to these rules, and one draw needn't show every extreme that they name: `tile_cols`: slot j of row g = b * 8 + q with key k (see steps) lies in section s = k // 8; its column tile is c * 8 + e with column block c = (b + q * 4 + s) mod 32 and 0 <= e < 8. Live slots name distinct tiles and are in order of key. Slots that are not live hold 0 and arbitrary tile values. `tile_ptr`: each row starts at 0 and never falls; its last entry, the live count, is at least 1 and equals 256 on some row of every draw; counts are skewed, most rows holding a quarter of 256 or less.
All inputs are finite; a program needn't handle non-finite values.
Results may differ from a plain program's by a relative error of at most 0.001.
Values may be sent and summed in bfloat16 or wider, within the bound.
No kernel may reach another device: no remote copies, remote signals or barrier semaphores. Data moves between devices by JAX's collectives and lax.ppermute only.
A program may use at most 64 MiB of HBM per device.

v0:
```python
import functools

import jax
import jax.numpy as jnp
from jax import lax
from jax.experimental import pallas as pl
from jax.experimental.pallas import tpu as pltpu
from jax.sharding import PartitionSpec as P


TB = 8
CENTRE = 2
MIB = 1 << 20


def moved(block, rows, reps, source):
    route = []
    for row in range(rows):
        for rep in range(reps):
            from_row, from_rep = source(row, rep)
            route.append((from_row % rows * reps + from_rep % reps, row * reps + rep))
    return lax.ppermute(block, ("rows", "reps"), route)


def dense_kernel(sections, cols, ptr, tiles, dense, sem):
    size = tiles.shape[1]
    dense[...] = jnp.zeros(dense.shape, dense.dtype)

    def tile_copy(slot, section, row, entry):
        where = dense.at[
            section, pl.ds(row * size, size), pl.ds(pl.multiple_of(entry * size, size), size)
        ]
        return pltpu.make_async_copy(tiles.at[slot], where, sem)

    for section in range(sections):
        for row in range(TB):
            key = section * TB + row

            def send(slot, carry, section=section, row=row):
                tile_copy(slot, section, row, lax.rem(cols[0, slot], TB)).start()
                return carry

            lax.fori_loop(ptr[0, key], ptr[0, key + 1], send, 0)

    def arrive(slot, carry):
        tile_copy(0, 0, 0, 0).wait()
        return carry

    lax.fori_loop(0, ptr[0, sections * TB], arrive, 0)


def dense_sections(sections, cols, ptr, tiles):
    size = tiles.shape[1]
    scalars = pl.BlockSpec(memory_space=pltpu.SMEM)
    return pl.pallas_call(
        functools.partial(dense_kernel, sections),
        out_shape=pltpu.VMEM((sections, TB * size, TB * size), tiles.dtype),
        in_specs=[scalars, scalars, pl.BlockSpec(memory_space=pl.ANY)],
        out_specs=pl.BlockSpec(memory_space=pltpu.VMEM),
        scratch_shapes=[pltpu.SemaphoreType.DMA],
        compiler_params=pltpu.CompilerParams(vmem_limit_bytes=12 * MIB),
        name="dense_sections",
    )(cols, ptr, pltpu.with_memory_space_constraint(tiles, pltpu.HBM))


def product_kernel(sections, chained, dense, *refs):
    feats = refs[: len(sections)]
    total = refs[-1]
    value = refs[len(sections)][...] if chained else None
    for at, section in enumerate(sections):
        part = jnp.dot(dense[section], feats[at][...], preferred_element_type=jnp.float32)
        value = part if value is None else value + part
    total[...] = value


def product_sum(sections, dense, feats, start=None):
    operands = [dense, *feats] + ([] if start is None else [start])
    operands = [pltpu.with_memory_space_constraint(x, pltpu.VMEM) for x in operands]
    whole = pl.BlockSpec(memory_space=pltpu.VMEM)
    return pl.pallas_call(
        functools.partial(product_kernel, sections, start is not None),
        out_shape=pltpu.VMEM((dense.shape[1], feats[0].shape[1]), jnp.float32),
        in_specs=[whole] * len(operands),
        out_specs=whole,
        compiler_params=pltpu.CompilerParams(vmem_limit_bytes=16 * MIB),
    )(*operands)


def body(features, tiles, tile_cols, tile_ptr):
    size = tiles.shape[1]
    width = features.shape[1]
    rows = lax.axis_size("rows")
    reps = lax.axis_size("reps")
    sections = rows // reps
    line = rows // 4

    def aligned(section):
        return lambda row, rep: (row + sections * rep + section, rep)

    def step(distance):
        return lambda row, rep: (row + distance, rep)

    def step_in_line(distance):
        def source(row, rep):
            base, at = row // line * line, row % line
            if 0 <= at + distance < line:
                return row + distance, rep
            turn = line // sections if distance > 0 else -(line // sections)
            return base + (at + distance) % line, rep + turn

        return source

    dense = dense_sections(sections, tile_cols, tile_ptr, tiles)
    centre = moved(features, rows, reps, aligned(CENTRE))
    first = moved(features, rows, reps, aligned(0))
    after = moved(centre, rows, reps, step(1))
    before = moved(centre, rows, reps, step_in_line(-1))
    partial = product_sum((CENTRE, 0), dense, (centre, first))
    partial = product_sum((CENTRE + 1, CENTRE - 1), dense, (after, before), partial)
    blocks = partial.reshape(reps, size, width)
    arrived = lax.all_to_all(blocks, "reps", split_axis=0, concat_axis=0, tiled=True)
    return arrived.sum(axis=0).astype(jnp.bfloat16)


def solution(mesh):
    placed = (
        P("rows", "cols"),
        P(("rows", "reps"), None, None),
        P(("rows", "reps"), None),
        P(("rows", "reps"), None),
    )
    return jax.shard_map(
        body, mesh=mesh, in_specs=placed, out_specs=P(("rows", "reps"), "cols"), check_vma=False
    )
```

profile of v0, /device:TPU:110, one launch (start us, length us, event | category | flops | bytes accessed | tf_op | source)
XLA Modules:
  0.0 91.1 jit_solution(11080605424012325980)
XLA Ops:
  0.0 4.2 %collective-permute-start = (bf16[1024,128]{1,0:T(8,128)(2,1)}, bf16[1024,128]{1,0:T(8,128)(2,1)S(1)}, u32[]{:S(2)}, u32[]{:S(2)}) collective-permute-start(bf16[1024,128]{1,0:T(8,128)(2,1)} %param.4), channel_id=1, source_target_pairs={{64,0},{193,1},{322,2},{451,3},{580,4},{709,5},{838,6},{967,7},{96... | collective-permute-start | bytes 786440 | tf_op jit(solution)/shard_map/ppermute | solution.py:22
  4.2 1.6 %collective-permute-start.3 = (bf16[1024,128]{1,0:T(8,128)(2,1)}, bf16[1024,128]{1,0:T(8,128)(2,1)S(1)}, u32[]{:S(2)}, u32[]{:S(2)}) collective-permute-start(bf16[1024,128]{1,0:T(8,128)(2,1)} %param.4), channel_id=1, source_target_pairs={{0,0},{129,1},{258,2},{387,3},{516,4},{645,5},{774,6},{903,7},{32,... | collective-permute-start | bytes 786440 | tf_op jit(solution)/shard_map/ppermute | solution.py:22
  5.8 14.3 %collective-permute-done.refs_0_ = bf16[1024,128]{1,0:T(8,128)(2,1)S(1)} collective-permute-done((bf16[1024,128]{1,0:T(8,128)(2,1)}, bf16[1024,128]{1,0:T(8,128)(2,1)S(1)}, u32[]{:S(2)}, u32[]{:S(2)}) %collective-permute-start) | collective-permute-done | bytes 262176 | tf_op jit(solution)/shard_map/ppermute | solution.py:22
  20.2 7.9 %collective-permute-start.2 = (bf16[1024,128]{1,0:T(8,128)(2,1)S(1)}, bf16[1024,128]{1,0:T(8,128)(2,1)S(1)}, u32[]{:S(2)}, u32[]{:S(2)}) collective-permute-start(bf16[1024,128]{1,0:T(8,128)(2,1)S(1)} %collective-permute-done.refs_0_), channel_id=1, source_target_pairs={{230,0},{231,1},{224,2},{225,3},{226,4},{227,5},{228,6},{229,7},{0... | collective-permute-start | bytes 786440 | tf_op jit(solution)/shard_map/ppermute | solution.py:22
  28.1 2.9 %collective-permute-start.1 = (bf16[1024,128]{1,0:T(8,128)(2,1)S(1)}, bf16[1024,128]{1,0:T(8,128)(2,1)S(1)}, u32[]{:S(2)}, u32[]{:S(2)}) collective-permute-start(bf16[1024,128]{1,0:T(8,128)(2,1)S(1)} %collective-permute-done.refs_0_), channel_id=1, source_target_pairs={{32,0},{33,1},{34,2},{35,3},{36,4},{37,5},{38,6},{39,7},{64,32},{6... | collective-permute-start | bytes 786440 | tf_op jit(solution)/shard_map/ppermute | solution.py:22
  31.0 0.0 copy-start
  31.0 0.7 copy-done
  31.7 0.0 copy-start.1
  31.7 0.7 copy-done.1
  32.3 2.5 %dense_sections.1.dense = bf16[4,1024,1024]{2,1,0:T(8,128)(2,1)S(1)} custom-call(s32[1,256]{1,0:T(1,128)S(1)} %copy-done, s32[1,33]{1,0:T(1,128)S(1)} %copy-done.1, bf16[256,128,128]{2,1,0:T(8,128)(2,1)} %tiles.1), custom_call_target="tpu_custom_call" | custom-call | tf_op jit(solution)/shard_map/dense_sections/pallas_call | solution.py:55
  34.8 0.0 collective-permute-done.3.refs_1_
  34.8 1.2 %shard_map.46.refs_2_ = f32[1024,128]{1,0:T(8,128)S(1)} custom-call(bf16[4,1024,1024]{2,1,0:T(8,128)(2,1)S(1)} %dense_sections.1.dense, bf16[1024,128]{1,0:T(8,128)(2,1)S(1)} %collective-permute-done.refs_0_, bf16[1024,128]{1,0:T(8,128)(2,1)S(1)} %collective-permute-done.3.refs_1_), custom_call_target="tpu_custom_call" | custom-call | tf_op jit(solution)/shard_map/pallas_call | solution.py:80
  36.1 0.0 collective-permute-done.2.refs_1_
  36.1 8.7 %collective-permute-done.1.refs_0_ = bf16[1024,128]{1,0:T(8,128)(2,1)S(1)} collective-permute-done((bf16[1024,128]{1,0:T(8,128)(2,1)S(1)}, bf16[1024,128]{1,0:T(8,128)(2,1)S(1)}, u32[]{:S(2)}, u32[]{:S(2)}) %collective-permute-start.1) | collective-permute-done | bytes 262176 | tf_op jit(solution)/shard_map/ppermute | solution.py:22
  44.8 1.2 %shard_map.47 = f32[1024,128]{1,0:T(8,128)S(1)} custom-call(bf16[4,1024,1024]{2,1,0:T(8,128)(2,1)S(1)} %dense_sections.1.dense, bf16[1024,128]{1,0:T(8,128)(2,1)S(1)} %collective-permute-done.1.refs_0_, bf16[1024,128]{1,0:T(8,128)(2,1)S(1)} %collective-permute-done.2.refs_1_, f32[1024,128]{1,0:T(8,128)S(1)} %shard_map.46.refs_2_), custom_call_target="tpu_custom_call" | custom-call | tf_op jit(solution)/shard_map/pallas_call | solution.py:80
  46.1 44.4 %all_to_all.5 = f32[8,128,128]{2,1,0:T(8,128)S(1)} all-to-all(f32[8,128,128]{2,1,0:T(8,128)S(1)} %bitcast.1), channel_id=1, replica_groups=mesh['rows'=32,'cols'=4,'reps'=8] {'reps'}, dimensions={0} | all-to-all | bytes 1048576 | tf_op jit(solution)/shard_map/all_to_all | solution.py:121
  90.5 0.6 reduce_sum.9
Async XLA Ops:
  0.0 20.2 %collective-permute-start = (bf16[1024,128]{1,0:T(8,128)(2,1)}, bf16[1024,128]{1,0:T(8,128)(2,1)S(1)}, u32[]{:S(2)}, u32[]{:S(2)}) collective-permute-start(bf16[1024,128]{1,0:T(8,128)(2,1)} %param.4), channel_id=1, source_target_pairs={{64,0},{193,1},{322,2},{451,3},{580,4},{709,5},{838,6},{967,7},{96... | collective-permute-start | bytes 786440 | tf_op jit(solution)/shard_map/ppermute | solution.py:22
  4.2 30.6 %collective-permute-start.3 = (bf16[1024,128]{1,0:T(8,128)(2,1)}, bf16[1024,128]{1,0:T(8,128)(2,1)S(1)}, u32[]{:S(2)}, u32[]{:S(2)}) collective-permute-start(bf16[1024,128]{1,0:T(8,128)(2,1)} %param.4), channel_id=1, source_target_pairs={{0,0},{129,1},{258,2},{387,3},{516,4},{645,5},{774,6},{903,7},{32,... | collective-permute-start | bytes 786440 | tf_op jit(solution)/shard_map/ppermute | solution.py:22
  20.2 15.9 %collective-permute-start.2 = (bf16[1024,128]{1,0:T(8,128)(2,1)S(1)}, bf16[1024,128]{1,0:T(8,128)(2,1)S(1)}, u32[]{:S(2)}, u32[]{:S(2)}) collective-permute-start(bf16[1024,128]{1,0:T(8,128)(2,1)S(1)} %collective-permute-done.refs_0_), channel_id=1, source_target_pairs={{230,0},{231,1},{224,2},{225,3},{226,4},{227,5},{228,6},{229,7},{0... | collective-permute-start | bytes 786440 | tf_op jit(solution)/shard_map/ppermute | solution.py:22
  28.1 16.8 %collective-permute-start.1 = (bf16[1024,128]{1,0:T(8,128)(2,1)S(1)}, bf16[1024,128]{1,0:T(8,128)(2,1)S(1)}, u32[]{:S(2)}, u32[]{:S(2)}) collective-permute-start(bf16[1024,128]{1,0:T(8,128)(2,1)S(1)} %collective-permute-done.refs_0_), channel_id=1, source_target_pairs={{32,0},{33,1},{34,2},{35,3},{36,4},{37,5},{38,6},{39,7},{64,32},{6... | collective-permute-start | bytes 786440 | tf_op jit(solution)/shard_map/ppermute | solution.py:22
  31.0 0.7 copy-start
  31.7 0.7 copy-start.1
where the time goes:
time: 91.6 us; the launch traced here: 91.1 us
  blocking collectives  44.4 us (48%)
  waiting for transfers between devices  23.1 us (25%)
  starting transfers between devices  16.6 us (18%)
  Pallas kernels  4.95 us (5%)
  local copies, waits for them, and re-layouts  1.33 us (1%)
    all_to_all x1, blocking collectives, body(): lax.all_to_all(blocks, 'reps', split_axis=0, concat_axis=0, tiled=True)  44.4 us
    ppermute x4, waiting for transfers between devices, moved(): return lax.ppermute(block, ('rows', 'reps'), route)  23.1 us
    ppermute x4, starting transfers between devices, moved(): return lax.ppermute(block, ('rows', 'reps'), route)  16.6 us
    pallas_call x2, Pallas kernels, product_sum(): pl.pallas_call(functools.partial(product_kernel, sections, start is not N...  2.49 us
    pallas_call x1, Pallas kernels, dense_sections(): pl.pallas_call(functools.partial(dense_kernel, sections), out_shape=pltpu...  2.46 us
  transfers between devices with their start and end apart: 4, of which 2 were waited for; matrix products, arithmetic and copies ran while one was open for 0% of the time, Pallas kernels for 4%

commit v1 on v0

--- a/solution.py
+++ b/solution.py
@@ -9,17 +9,23 @@
 
 
 TB = 8
-CENTRE = 2
+ACROSS = 5
 MIB = 1 << 20
 
 
-def moved(block, rows, reps, source):
+def moved(block, sizes, source):
+    rows, cols, reps = sizes
+
+    def device(row, col, rep):
+        return (row % rows * cols + col) * reps + rep % reps
+
     route = []
     for row in range(rows):
-        for rep in range(reps):
-            from_row, from_rep = source(row, rep)
-            route.append((from_row % rows * reps + from_rep % reps, row * reps + rep))
-    return lax.ppermute(block, ("rows", "reps"), route)
+        for col in range(cols):
+            for rep in range(reps):
+                from_row, from_rep = source(row, col, rep)
+                route.append((device(from_row, col, from_rep), device(row, col, rep)))
+    return lax.ppermute(block, ("rows", "cols", "reps"), route)
 
 
 def dense_kernel(sections, cols, ptr, tiles, dense, sem):
@@ -89,34 +95,26 @@
 def body(features, tiles, tile_cols, tile_ptr):
     size = tiles.shape[1]
     width = features.shape[1]
-    rows = lax.axis_size("rows")
-    reps = lax.axis_size("reps")
+    sizes = [lax.axis_size(axis) for axis in ("rows", "cols", "reps")]
+    rows, _, reps = sizes
     sections = rows // reps
-    line = rows // 4
 
-    def aligned(section):
-        return lambda row, rep: (row + sections * rep + section, rep)
-
-    def step(distance):
-        return lambda row, rep: (row + distance, rep)
-
-    def step_in_line(distance):
-        def source(row, rep):
-            base, at = row // line * line, row % line
-            if 0 <= at + distance < line:
-                return row + distance, rep
-            turn = line // sections if distance > 0 else -(line // sections)
-            return base + (at + distance) % line, rep + turn
+    def owner(section):
+        def source(row, col, rep):
+            across = (col + section) % 2 == 1
+            return row + sections * rep + section, rep ^ ACROSS if across else rep
 
         return source
 
     dense = dense_sections(sections, tile_cols, tile_ptr, tiles)
-    centre = moved(features, rows, reps, aligned(CENTRE))
-    first = moved(features, rows, reps, aligned(0))
-    after = moved(centre, rows, reps, step(1))
-    before = moved(centre, rows, reps, step_in_line(-1))
-    partial = product_sum((CENTRE, 0), dense, (centre, first))
-    partial = product_sum((CENTRE + 1, CENTRE - 1), dense, (after, before), partial)
+    feats = []
+    for section in range(sections):
+        feats.append(moved(features, sizes, owner(section)))
+    half = sections // 2
+    partial = None
+    for begin in (0, half):
+        chosen = tuple(range(begin, begin + half))
+        partial = product_sum(chosen, dense, feats[begin : begin + half], partial)
     blocks = partial.reshape(reps, size, width)
     arrived = lax.all_to_all(blocks, "reps", split_axis=0, concat_axis=0, tiled=True)
     return arrived.sum(axis=0).astype(jnp.bfloat16)

time: 91.6 us -> 111 us (1.21)
  the two profiles are of different devices: /device:TPU:110 before, /device:TPU:120 now
where the time goes in v1:
time: 111 us; the launch traced here: 110 us
  blocking collectives  60.7 us (55%)
  starting transfers between devices  27.2 us (25%)
  waiting for transfers between devices  14.2 us (13%)
  Pallas kernels  5.96 us (5%)
  local copies, waits for them, and re-layouts  1.33 us (1%)
    all_to_all x1, blocking collectives, body(): lax.all_to_all(blocks, 'reps', split_axis=0, concat_axis=0, tiled=True)  60.7 us
    ppermute x4, starting transfers between devices, moved(): return lax.ppermute(block, ('rows', 'cols', 'reps'), route)  27.2 us
    ppermute x4, waiting for transfers between devices, moved(): return lax.ppermute(block, ('rows', 'cols', 'reps'), route)  14.2 us
    pallas_call x1, Pallas kernels, dense_sections(): pl.pallas_call(functools.partial(dense_kernel, sections), out_shape=pltpu...  3.47 us
    pallas_call x2, Pallas kernels, product_sum(): pl.pallas_call(functools.partial(product_kernel, sections, start is not N...  2.49 us
  transfers between devices with their start and end apart: 4, of which 2 were waited for; matrix products, arithmetic and copies ran while one was open for 0% of the time, Pallas kernels for 4%

profile of v1, /device:TPU:120, one launch (start us, length us, event | category | flops | bytes accessed | tf_op | source)
XLA Modules:
  0.0 110.1 jit_solution(17401063392330328532)
XLA Ops:
  0.0 15.1 %collective-permute-start.3 = (bf16[1024,128]{1,0:T(8,128)(2,1)}, bf16[1024,128]{1,0:T(8,128)(2,1)S(1)}, u32[]{:S(2)}, u32[]{:S(2)}) collective-permute-start(bf16[1024,128]{1,0:T(8,128)(2,1)} %param.4), channel_id=1, source_target_pairs={{37,0},{164,1},{295,2},{422,3},{545,4},{672,5},{803,6},{930,7},{40... | collective-permute-start | bytes 786440 | tf_op jit(solution)/shard_map/ppermute | solution.py:28
  15.1 1.6 %collective-permute-start.2 = (bf16[1024,128]{1,0:T(8,128)(2,1)}, bf16[1024,128]{1,0:T(8,128)(2,1)S(1)}, u32[]{:S(2)}, u32[]{:S(2)}) collective-permute-start(bf16[1024,128]{1,0:T(8,128)(2,1)} %param.4), channel_id=1, source_target_pairs={{0,0},{129,1},{258,2},{387,3},{516,4},{645,5},{774,6},{903,7},{13,... | collective-permute-start | bytes 786440 | tf_op jit(solution)/shard_map/ppermute | solution.py:28
  16.7 8.3 %collective-permute-start.1 = (bf16[1024,128]{1,0:T(8,128)(2,1)}, bf16[1024,128]{1,0:T(8,128)(2,1)S(1)}, u32[]{:S(2)}, u32[]{:S(2)}) collective-permute-start(bf16[1024,128]{1,0:T(8,128)(2,1)} %param.4), channel_id=1, source_target_pairs={{101,0},{228,1},{359,2},{486,3},{609,4},{736,5},{867,6},{994,7},{1... | collective-permute-start | bytes 786440 | tf_op jit(solution)/shard_map/ppermute | solution.py:28
  25.0 2.2 %collective-permute-start = (bf16[1024,128]{1,0:T(8,128)(2,1)}, bf16[1024,128]{1,0:T(8,128)(2,1)S(1)}, u32[]{:S(2)}, u32[]{:S(2)}) collective-permute-start(bf16[1024,128]{1,0:T(8,128)(2,1)} %param.4), channel_id=1, source_target_pairs={{64,0},{193,1},{322,2},{451,3},{580,4},{709,5},{838,6},{967,7},{77... | collective-permute-start | bytes 786440 | tf_op jit(solution)/shard_map/ppermute | solution.py:28
  27.2 0.0 copy-start
  27.2 0.7 copy-done
  27.9 0.0 copy-start.1
  27.9 0.7 copy-done.1
  28.6 3.5 %dense_sections.1.dense = bf16[4,1024,1024]{2,1,0:T(8,128)(2,1)S(1)} custom-call(s32[1,256]{1,0:T(1,128)S(1)} %copy-done, s32[1,33]{1,0:T(1,128)S(1)} %copy-done.1, bf16[256,128,128]{2,1,0:T(8,128)(2,1)} %tiles.1), custom_call_target="tpu_custom_call" | custom-call | tf_op jit(solution)/shard_map/dense_sections/pallas_call | solution.py:61
  32.1 0.0 collective-permute-done.3.refs_1_
  32.1 0.0 collective-permute-done.2.refs_0_
  32.1 1.2 %shard_map.46.refs_2_ = f32[1024,128]{1,0:T(8,128)S(1)} custom-call(bf16[4,1024,1024]{2,1,0:T(8,128)(2,1)S(1)} %dense_sections.1.dense, bf16[1024,128]{1,0:T(8,128)(2,1)S(1)} %collective-permute-done.2.refs_0_, bf16[1024,128]{1,0:T(8,128)(2,1)S(1)} %collective-permute-done.3.refs_1_), custom_call_target="tpu_custom_call" | custom-call | tf_op jit(solution)/shard_map/pallas_call | solution.py:86
  33.3 10.0 %collective-permute-done.1.refs_1_ = bf16[1024,128]{1,0:T(8,128)(2,1)S(1)} collective-permute-done((bf16[1024,128]{1,0:T(8,128)(2,1)}, bf16[1024,128]{1,0:T(8,128)(2,1)S(1)}, u32[]{:S(2)}, u32[]{:S(2)}) %collective-permute-start.1) | collective-permute-done | bytes 262176 | tf_op jit(solution)/shard_map/ppermute | solution.py:28
  43.4 4.1 %collective-permute-done.refs_0_ = bf16[1024,128]{1,0:T(8,128)(2,1)S(1)} collective-permute-done((bf16[1024,128]{1,0:T(8,128)(2,1)}, bf16[1024,128]{1,0:T(8,128)(2,1)S(1)}, u32[]{:S(2)}, u32[]{:S(2)}) %collective-permute-start) | collective-permute-done | bytes 262176 | tf_op jit(solution)/shard_map/ppermute | solution.py:28
  47.5 1.2 %shard_map.47 = f32[1024,128]{1,0:T(8,128)S(1)} custom-call(bf16[4,1024,1024]{2,1,0:T(8,128)(2,1)S(1)} %dense_sections.1.dense, bf16[1024,128]{1,0:T(8,128)(2,1)S(1)} %collective-permute-done.refs_0_, bf16[1024,128]{1,0:T(8,128)(2,1)S(1)} %collective-permute-done.1.refs_1_, f32[1024,128]{1,0:T(8,128)S(1)} %shard_map.46.refs_2_), custom_call_target="tpu_custom_call" | custom-call | tf_op jit(solution)/shard_map/pallas_call | solution.py:86
  48.8 60.7 %all_to_all.5 = f32[8,128,128]{2,1,0:T(8,128)S(1)} all-to-all(f32[8,128,128]{2,1,0:T(8,128)S(1)} %bitcast.1), channel_id=1, replica_groups=mesh['rows'=32,'cols'=4,'reps'=8] {'reps'}, dimensions={0} | all-to-all | bytes 1048576 | tf_op jit(solution)/shard_map/all_to_all | solution.py:119
  109.5 0.6 reduce_sum.9
Async XLA Ops:
  0.0 32.1 %collective-permute-start.3 = (bf16[1024,128]{1,0:T(8,128)(2,1)}, bf16[1024,128]{1,0:T(8,128)(2,1)S(1)}, u32[]{:S(2)}, u32[]{:S(2)}) collective-permute-start(bf16[1024,128]{1,0:T(8,128)(2,1)} %param.4), channel_id=1, source_target_pairs={{37,0},{164,1},{295,2},{422,3},{545,4},{672,5},{803,6},{930,7},{40... | collective-permute-start | bytes 786440 | tf_op jit(solution)/shard_map/ppermute | solution.py:28
  15.1 17.0 %collective-permute-start.2 = (bf16[1024,128]{1,0:T(8,128)(2,1)}, bf16[1024,128]{1,0:T(8,128)(2,1)S(1)}, u32[]{:S(2)}, u32[]{:S(2)}) collective-permute-start(bf16[1024,128]{1,0:T(8,128)(2,1)} %param.4), channel_id=1, source_target_pairs={{0,0},{129,1},{258,2},{387,3},{516,4},{645,5},{774,6},{903,7},{13,... | collective-permute-start | bytes 786440 | tf_op jit(solution)/shard_map/ppermute | solution.py:28
  16.7 26.7 %collective-permute-start.1 = (bf16[1024,128]{1,0:T(8,128)(2,1)}, bf16[1024,128]{1,0:T(8,128)(2,1)S(1)}, u32[]{:S(2)}, u32[]{:S(2)}) collective-permute-start(bf16[1024,128]{1,0:T(8,128)(2,1)} %param.4), channel_id=1, source_target_pairs={{101,0},{228,1},{359,2},{486,3},{609,4},{736,5},{867,6},{994,7},{1... | collective-permute-start | bytes 786440 | tf_op jit(solution)/shard_map/ppermute | solution.py:28
  25.0 22.5 %collective-permute-start = (bf16[1024,128]{1,0:T(8,128)(2,1)}, bf16[1024,128]{1,0:T(8,128)(2,1)S(1)}, u32[]{:S(2)}, u32[]{:S(2)}) collective-permute-start(bf16[1024,128]{1,0:T(8,128)(2,1)} %param.4), channel_id=1, source_target_pairs={{64,0},{193,1},{322,2},{451,3},{580,4},{709,5},{838,6},{967,7},{77... | collective-permute-start | bytes 786440 | tf_op jit(solution)/shard_map/ppermute | solution.py:28
  27.2 0.7 copy-start
  27.9 0.7 copy-start.1

commit v2 on v1

--- a/solution.py
+++ b/solution.py
@@ -10,6 +10,7 @@
 
 TB = 8
 ACROSS = 5
+CENTRE = 2
 MIB = 1 << 20
 
 
@@ -99,22 +100,33 @@
     rows, _, reps = sizes
     sections = rows // reps
 
-    def owner(section):
+    line = rows // 4
+
+    def owner(section, crossing):
         def source(row, col, rep):
-            across = (col + section) % 2 == 1
+            across = col % 2 == crossing
             return row + sections * rep + section, rep ^ ACROSS if across else rep
 
         return source
 
+    def neighbour(distance, turning):
+        turn = distance * line // sections
+
+        def source(row, col, rep):
+            at = row % line + distance
+            if col % 2 == turning and not 0 <= at < line:
+                return row - row % line + at % line, rep + turn
+            return row + distance, rep
+
+        return source
+
     dense = dense_sections(sections, tile_cols, tile_ptr, tiles)
-    feats = []
-    for section in range(sections):
-        feats.append(moved(features, sizes, owner(section)))
-    half = sections // 2
-    partial = None
-    for begin in (0, half):
-        chosen = tuple(range(begin, begin + half))
-        partial = product_sum(chosen, dense, feats[begin : begin + half], partial)
+    centre = moved(features, sizes, owner(CENTRE, 1))
+    first = moved(features, sizes, owner(0, 0))
+    after = moved(centre, sizes, neighbour(1, 0))
+    before = moved(centre, sizes, neighbour(-1, 1))
+    partial = product_sum((CENTRE, 0), dense, (centre, first))
+    partial = product_sum((CENTRE + 1, CENTRE - 1), dense, (after, before), partial)
     blocks = partial.reshape(reps, size, width)
     arrived = lax.all_to_all(blocks, "reps", split_axis=0, concat_axis=0, tiled=True)
     return arrived.sum(axis=0).astype(jnp.bfloat16)

time: 111 us -> 79.1 us (0.71)
  the two profiles are of different devices: /device:TPU:120 before, /device:TPU:118 now
where the time goes in v2:
time: 79.1 us; the launch traced here: 78.7 us
  blocking collectives  35.1 us (44%)
  starting transfers between devices  31.1 us (39%)
  Pallas kernels  5.99 us (8%)
  waiting for transfers between devices  4.54 us (6%)
  local copies, waits for them, and re-layouts  1.33 us (2%)
    all_to_all x1, blocking collectives, body(): lax.all_to_all(blocks, 'reps', split_axis=0, concat_axis=0, tiled=True)  35.1 us
    ppermute x4, starting transfers between devices, moved(): return lax.ppermute(block, ('rows', 'cols', 'reps'), route)  31.1 us
    ppermute x4, waiting for transfers between devices, moved(): return lax.ppermute(block, ('rows', 'cols', 'reps'), route)  4.54 us
    pallas_call x1, Pallas kernels, dense_sections(): pl.pallas_call(functools.partial(dense_kernel, sections), out_shape=pltpu...  3.5 us
    pallas_call x2, Pallas kernels, product_sum(): pl.pallas_call(functools.partial(product_kernel, sections, start is not N...  2.49 us
  transfers between devices with their start and end apart: 4, of which 2 were waited for; matrix products, arithmetic and copies ran while one was open for 0% of the time, Pallas kernels for 6%

profile of v2, /device:TPU:118, one launch (start us, length us, event | category | flops | bytes accessed | tf_op | source)
XLA Modules:
  0.0 78.7 jit_solution(7813653670884732290)
XLA Ops:
  0.0 2.4 %collective-permute-start = (bf16[1024,128]{1,0:T(8,128)(2,1)}, bf16[1024,128]{1,0:T(8,128)(2,1)S(1)}, u32[]{:S(2)}, u32[]{:S(2)}) collective-permute-start(bf16[1024,128]{1,0:T(8,128)(2,1)} %param.4), channel_id=1, source_target_pairs={{64,0},{193,1},{322,2},{451,3},{580,4},{709,5},{838,6},{967,7},{77... | collective-permute-start | bytes 786440 | tf_op jit(solution)/shard_map/ppermute | solution.py:29
  2.4 22.8 %collective-permute-start.3 = (bf16[1024,128]{1,0:T(8,128)(2,1)}, bf16[1024,128]{1,0:T(8,128)(2,1)S(1)}, u32[]{:S(2)}, u32[]{:S(2)}) collective-permute-start(bf16[1024,128]{1,0:T(8,128)(2,1)} %param.4), channel_id=1, source_target_pairs={{5,0},{132,1},{263,2},{390,3},{513,4},{640,5},{771,6},{898,7},{8,8... | collective-permute-start | bytes 786440 | tf_op jit(solution)/shard_map/ppermute | solution.py:29
  25.3 0.0 collective-permute-done.refs_0_
  25.3 3.4 %collective-permute-start.2 = (bf16[1024,128]{1,0:T(8,128)(2,1)S(1)}, bf16[1024,128]{1,0:T(8,128)(2,1)S(1)}, u32[]{:S(2)}, u32[]{:S(2)}) collective-permute-start(bf16[1024,128]{1,0:T(8,128)(2,1)S(1)} %collective-permute-done.refs_0_), channel_id=1, source_target_pairs={{992,0},{993,1},{994,2},{995,3},{996,4},{997,5},{998,6},{999,7},{2... | collective-permute-start | bytes 786440 | tf_op jit(solution)/shard_map/ppermute | solution.py:29
  28.7 2.4 %collective-permute-start.1 = (bf16[1024,128]{1,0:T(8,128)(2,1)S(1)}, bf16[1024,128]{1,0:T(8,128)(2,1)S(1)}, u32[]{:S(2)}, u32[]{:S(2)}) collective-permute-start(bf16[1024,128]{1,0:T(8,128)(2,1)S(1)} %collective-permute-done.refs_0_), channel_id=1, source_target_pairs={{32,0},{33,1},{34,2},{35,3},{36,4},{37,5},{38,6},{39,7},{40,8},{41... | collective-permute-start | bytes 786440 | tf_op jit(solution)/shard_map/ppermute | solution.py:29
  31.1 0.0 copy-start
  31.1 0.7 copy-done
  31.8 0.0 copy-start.1
  31.8 0.7 copy-done.1
  32.5 3.5 %dense_sections.1.dense = bf16[4,1024,1024]{2,1,0:T(8,128)(2,1)S(1)} custom-call(s32[1,256]{1,0:T(1,128)S(1)} %copy-done, s32[1,33]{1,0:T(1,128)S(1)} %copy-done.1, bf16[256,128,128]{2,1,0:T(8,128)(2,1)} %tiles.1), custom_call_target="tpu_custom_call" | custom-call | tf_op jit(solution)/shard_map/dense_sections/pallas_call | solution.py:62
  36.0 0.0 collective-permute-done.3.refs_1_
  36.0 1.2 %shard_map.46.refs_2_ = f32[1024,128]{1,0:T(8,128)S(1)} custom-call(bf16[4,1024,1024]{2,1,0:T(8,128)(2,1)S(1)} %dense_sections.1.dense, bf16[1024,128]{1,0:T(8,128)(2,1)S(1)} %collective-permute-done.refs_0_, bf16[1024,128]{1,0:T(8,128)(2,1)S(1)} %collective-permute-done.3.refs_1_), custom_call_target="tpu_custom_call" | custom-call | tf_op jit(solution)/shard_map/pallas_call | solution.py:87
  37.2 1.0 %collective-permute-done.2.refs_1_ = bf16[1024,128]{1,0:T(8,128)(2,1)S(1)} collective-permute-done((bf16[1024,128]{1,0:T(8,128)(2,1)S(1)}, bf16[1024,128]{1,0:T(8,128)(2,1)S(1)}, u32[]{:S(2)}, u32[]{:S(2)}) %collective-permute-start.2) | collective-permute-done | bytes 262176 | tf_op jit(solution)/shard_map/ppermute | solution.py:29
  38.2 3.6 %collective-permute-done.1.refs_0_ = bf16[1024,128]{1,0:T(8,128)(2,1)S(1)} collective-permute-done((bf16[1024,128]{1,0:T(8,128)(2,1)S(1)}, bf16[1024,128]{1,0:T(8,128)(2,1)S(1)}, u32[]{:S(2)}, u32[]{:S(2)}) %collective-permute-start.1) | collective-permute-done | bytes 262176 | tf_op jit(solution)/shard_map/ppermute | solution.py:29
  41.8 1.2 %shard_map.47 = f32[1024,128]{1,0:T(8,128)S(1)} custom-call(bf16[4,1024,1024]{2,1,0:T(8,128)(2,1)S(1)} %dense_sections.1.dense, bf16[1024,128]{1,0:T(8,128)(2,1)S(1)} %collective-permute-done.1.refs_0_, bf16[1024,128]{1,0:T(8,128)(2,1)S(1)} %collective-permute-done.2.refs_1_, f32[1024,128]{1,0:T(8,128)S(1)} %shard_map.46.refs_2_), custom_call_target="tpu_custom_call" | custom-call | tf_op jit(solution)/shard_map/pallas_call | solution.py:87
  43.0 35.1 %all_to_all.5 = f32[8,128,128]{2,1,0:T(8,128)S(1)} all-to-all(f32[8,128,128]{2,1,0:T(8,128)S(1)} %bitcast.1), channel_id=1, replica_groups=mesh['rows'=32,'cols'=4,'reps'=8] {'reps'}, dimensions={0} | all-to-all | bytes 1048576 | tf_op jit(solution)/shard_map/all_to_all | solution.py:131
  78.1 0.6 reduce_sum.9
Async XLA Ops:
  0.0 25.3 %collective-permute-start = (bf16[1024,128]{1,0:T(8,128)(2,1)}, bf16[1024,128]{1,0:T(8,128)(2,1)S(1)}, u32[]{:S(2)}, u32[]{:S(2)}) collective-permute-start(bf16[1024,128]{1,0:T(8,128)(2,1)} %param.4), channel_id=1, source_target_pairs={{64,0},{193,1},{322,2},{451,3},{580,4},{709,5},{838,6},{967,7},{77... | collective-permute-start | bytes 786440 | tf_op jit(solution)/shard_map/ppermute | solution.py:29
  2.4 33.6 %collective-permute-start.3 = (bf16[1024,128]{1,0:T(8,128)(2,1)}, bf16[1024,128]{1,0:T(8,128)(2,1)S(1)}, u32[]{:S(2)}, u32[]{:S(2)}) collective-permute-start(bf16[1024,128]{1,0:T(8,128)(2,1)} %param.4), channel_id=1, source_target_pairs={{5,0},{132,1},{263,2},{390,3},{513,4},{640,5},{771,6},{898,7},{8,8... | collective-permute-start | bytes 786440 | tf_op jit(solution)/shard_map/ppermute | solution.py:29
  25.3 12.9 %collective-permute-start.2 = (bf16[1024,128]{1,0:T(8,128)(2,1)S(1)}, bf16[1024,128]{1,0:T(8,128)(2,1)S(1)}, u32[]{:S(2)}, u32[]{:S(2)}) collective-permute-start(bf16[1024,128]{1,0:T(8,128)(2,1)S(1)} %collective-permute-done.refs_0_), channel_id=1, source_target_pairs={{992,0},{993,1},{994,2},{995,3},{996,4},{997,5},{998,6},{999,7},{2... | collective-permute-start | bytes 786440 | tf_op jit(solution)/shard_map/ppermute | solution.py:29
  28.7 13.1 %collective-permute-start.1 = (bf16[1024,128]{1,0:T(8,128)(2,1)S(1)}, bf16[1024,128]{1,0:T(8,128)(2,1)S(1)}, u32[]{:S(2)}, u32[]{:S(2)}) collective-permute-start(bf16[1024,128]{1,0:T(8,128)(2,1)S(1)} %collective-permute-done.refs_0_), channel_id=1, source_target_pairs={{32,0},{33,1},{34,2},{35,3},{36,4},{37,5},{38,6},{39,7},{40,8},{41... | collective-permute-start | bytes 786440 | tf_op jit(solution)/shard_map/ppermute | solution.py:29
  31.1 0.7 copy-start
  31.8 0.7 copy-start.1
